TPU v7x, 512 devices: a whole 4x4x16 slice. The times are simulated.
512 devices in a mesh: grp: 16 (over z), cand: 32 (over y, x, core).
Axes of the slice: x: 4, y: 4, z: 16, core: 2. Of those that a mesh axis runs over, the one named last changes fastest.
Arguments:
- embeddings: bfloat16 [384, 1024, 1024], P('grp', 'cand'), may hold values from -6 to 6
- hidden_weight: bfloat16 [2048, 1024], P('cand'), may hold values from -0.1875 to 0.1875
- score_weight: bfloat16 [2048], replicated, may hold values from -0.5 to 0.5
- relevance: int32 [384, 1024], P('grp', 'cand'), may hold values from 0 to 4
- rank_pos: int32 [384, 1024], P('grp', 'cand'), may hold values from 0 to 1023, as said below
- ideal_dcg: float32 [384], P('grp'), may hold values from 32 to 128
Outputs:
- grad_hidden: float32 [2048, 1024], P('cand')
- lambdas: float32 [384, 1024], P('grp', 'cand')
Inputs may be any that keep to these rules, and one draw needn't show every extreme that they name: `rank_pos`: in each group the rank positions are a permutation of 0 to 1023.
All inputs are finite; a program needn't handle non-finite values.
Results may differ from a plain program's by a relative error of at most 0.006.
Values may be sent and summed in bfloat16 or wider, within the bound.
No kernel may reach another device: no remote copies, remote signals or barrier semaphores. Data moves between devices by JAX's collectives and lax.ppermute only.
A program may use at most 64 MiB of HBM per device.

v0:
```python
import jax
import jax.numpy as jnp
from jax import lax
from jax.sharding import PartitionSpec as P

EPS = 1e-06


def turned_gather(arrays, axis, dims):
    turned = [jnp.moveaxis(a, dim, 0) for a, dim in zip(arrays, dims)]
    widths = [t[0].size for t in turned]
    both = jnp.concatenate([t.reshape(-1, w) for t, w in zip(turned, widths)], axis=1)
    result = lax.all_gather(both, axis, axis=0, tiled=True)
    parts = jnp.split(result, [sum(widths[:k]) for k in range(1, len(widths))], axis=1)
    return tuple(
        (
            jnp.moveaxis(b.reshape(-1, *t.shape[1:]), 0, dim)
            for b, t, dim in zip(parts, turned, dims)
        )
    )


def copy_for_each(value, axis):
    copies = jnp.broadcast_to(value, (lax.axis_size(axis), *value.shape))
    return lax.all_to_all(copies, axis, split_axis=0, concat_axis=0, tiled=True)


def joined_along(parts, dim):
    parts = jnp.moveaxis(parts, 0, dim)
    shape = parts.shape
    return parts.reshape(*shape[:dim], shape[dim] * shape[dim + 1], *shape[dim + 2 :])


def gathered_copies(value, axis, dim):
    parts = copy_for_each(value, axis)
    return joined_along(parts, dim)


def over_copies(value, axis):
    return copy_for_each(value, axis).sum(axis=0)


def pair_lambdas(own_score, own_gain, own_disc, far_score, far_gain, far_disc, ideal):
    gain_diff = far_gain[..., None, :] - own_gain[..., :, None]
    toward = jnp.sign(gain_diff)
    weight = (
        jnp.abs(gain_diff)
        * jnp.abs(far_disc[..., None, :] - own_disc[..., :, None])
        / ideal[..., None, None]
    )
    margin = own_score[..., :, None] - far_score[..., None, :]
    return jnp.sum(weight * toward * jax.nn.sigmoid(toward * margin), axis=-1)


def gain_of(labels):
    return jnp.exp2(labels.astype(jnp.float32)) - 1.0


def discount_of(positions):
    return 1.0 / jnp.log2(2.0 + positions.astype(jnp.float32))


def per_device(embeddings, hidden_weight, score_weight, relevance, rank_pos, ideal_dcg):
    grp_count, local, width = embeddings.shape
    cand_rows = embeddings.reshape(grp_count * local, width)
    all_labels, all_ranks = turned_gather((relevance, rank_pos), "cand", (1, 1))
    all_gain = gain_of(all_labels)
    all_disc = discount_of(all_ranks)
    pre_act = lax.dot_general(
        cand_rows,
        lax.all_gather(hidden_weight, "cand", axis=0, tiled=True),
        (((1,), (1,)), ((), ())),
        preferred_element_type=jnp.float32,
    )
    acts, pull = jax.vjp(jax.nn.gelu, pre_act)
    scores = jnp.dot(
        acts.astype(jnp.bfloat16), score_weight, preferred_element_type=jnp.float32
    ).reshape(grp_count, local)
    gain_vals = gain_of(relevance)
    discount = discount_of(rank_pos)
    lambdas = pair_lambdas(
        scores,
        gain_vals,
        discount,
        gathered_copies(scores, "cand", 1),
        all_gain,
        all_disc,
        ideal_dcg,
    )
    upstream = (
        lambdas.reshape(grp_count * local)[:, None] * score_weight.astype(jnp.float32)[None, :]
    )
    grad_pre = pull(upstream)[0].astype(jnp.bfloat16)
    owned = lax.psum_scatter(
        lax.dot_general(
            grad_pre, cand_rows, (((0,), (0,)), ((), ())), preferred_element_type=jnp.float32
        ).astype(jnp.bfloat16),
        "cand",
        scatter_dimension=0,
        tiled=True,
    ).astype(jnp.float32)
    summed = lax.psum(owned, "grp")
    squares = over_copies(jnp.sum(summed * summed), "cand")
    entries = summed.shape[0] * summed.shape[1] * lax.axis_size("cand")
    scale = lax.rsqrt(squares / entries + EPS)
    return (summed * scale, lambdas)


def solution(mesh):
    return jax.shard_map(
        per_device,
        mesh=mesh,
        in_specs=(
            P("grp", "cand", None),
            P("cand", None),
            P(),
            P("grp", "cand"),
            P("grp", "cand"),
            P("grp"),
        ),
        out_specs=(P("cand", None), P("grp", "cand")),
        check_vma=False,
    )
```

profile of v0, /device:TPU:1, one launch (start us, length us, event | category | flops | bytes accessed | tf_op | source)
XLA Modules:
  0.0 302.9 jit_solution(5547443069772350048)
XLA Ops:
  7.2 0.7 all-gather.2.cloned.1.call-update
  7.9 0.7 reshape.20
  8.6 0.8 copy.28
  9.4 0.8 copy.29
  10.2 0.1 pad_add_fusion
  10.2 28.5 %all_gather.6 = s32[1024,48]{1,0:T(8,128)S(1)} all-gather(s32[32,48]{1,0:T(8,128)S(1)} %pad_add_fusion), channel_id=1, replica_groups=mesh['grp'=16,'cand'=32] {'cand'}, dimensions={0}, use_global_device_ids=true | all-gather | bytes 202752 | tf_op jit(solution)/shard_map/all_gather | solution.py:13
  38.7 0.2 fusion.33
  38.9 0.2 copy.35
  39.1 0.2 copy.36
  39.3 38.9 %all-gather.2.cloned.1.call-done = bf16[2048,1024]{1,0:T(8,128)(2,1)} async-done(((bf16[64,1024]{1,0:T(8,128)(2,1)}), bf16[2048,1024]{1,0:T(8,128)(2,1)}) %all-gather.2.cloned.1.call-update) | async-done | bytes 4194320 | tf_op jit(solution)/shard_map/all_gather | solution.py:71
  78.2 5.3 %fusion.34 = f32[768,2048]{1,0:T(8,128)S(1)} fusion(bf16[768,1024]{1,0:T(8,128)(2,1)S(1)} %bitcast.12, bf16[2048,1024]{1,0:T(8,128)(2,1)} %all-gather.2.cloned.1.call-done), kind=kOutput, calls=%fused_computation.48 | convolution fusion | flops 3221225472 | bytes 12058624 | tf_op jit(solution)/shard_map/dot_general | solution.py:69
  83.5 2.7 copy-done.6
  86.1 2.2 fusion.22
  88.4 0.1 sub.63
  88.5 0.8 reshape.24
  89.3 5.3 %all-to-all-start = ((f32[32,1,768]{2,1,0:T(1,128)}), f32[32,1,768]{2,1,0:T(1,128)S(1)}, u32[]{:S(2)}, u32[]{:S(2)}) async-start(f32[32,1,768]{2,1,0:T(1,128)} %reshape.24), calls=%async_computation | async-start | bytes 196608 | tf_op jit(solution)/shard_map/all_to_all | solution.py:25
  94.7 7.3 %all-to-all-done = f32[32,1,768]{2,1,0:T(1,128)S(1)} async-done(((f32[32,1,768]{2,1,0:T(1,128)}), f32[32,1,768]{2,1,0:T(1,128)S(1)}, u32[]{:S(2)}, u32[]{:S(2)}) %all-to-all-start) | async-done | bytes 98336 | tf_op jit(solution)/shard_map/all_to_all | solution.py:25
  102.0 0.5 broadcast.84
  102.5 0.9 reduce.3
  103.4 0.1 reshape.25
  103.6 0.1 copy.32
  103.6 0.2 sub.65
  103.8 3.0 fusion.13
  106.8 0.1 mul.88
  106.9 10.4 %convolution_convert_fusion = bf16[2048,1024]{1,0:T(8,128)(2,1)} fusion(bf16[768,1024]{1,0:T(8,128)(2,1)S(1)} %bitcast.13, f32[768,2048]{1,0:T(8,128)} %copy-done.6, f32[2048]{0:T(1024)S(1)} %convert_element_type.34, f32[768]{0:T(1024)S(1)} %mul.88), kind=kOutput, calls=%fused_computation.19 | convolution fusion | flops 3256352768 | bytes 12069888 | tf_op jit(solution)/shard_map/dot_general | solution.py:95
  117.3 101.5 %reduce-scatter.2.cloned.1.call-done = bf16[64,1024]{1,0:T(8,128)(2,1)} async-done(((bf16[2048,1024]{1,0:T(8,128)(2,1)}), bf16[64,1024]{1,0:T(8,128)(2,1)}) %reduce-scatter.2.cloned.1.call-update) | async-done | bytes 131088 | tf_op jit(solution)/shard_map/reduce_scatter | solution.py:94
  218.8 46.8 %all-reduce.1 = f32[64,1024]{1,0:T(8,128)S(1)} all-reduce(bf16[64,1024]{1,0:T(8,128)(2,1)} %reduce-scatter.2.cloned.1.call-done), channel_id=1, replica_groups=mesh['grp'=16,'cand'=32] {'grp'}, use_global_device_ids=true, to_apply=%region_2.0 | all-reduce | flops 65536 | bytes 393216 | tf_op jit(solution)/shard_map/psum | solution.py:102
  265.6 0.7 multiply_reduce_fusion
  266.2 0.7 broadcast_in_dim.5
  266.9 27.1 %all_to_all.11 = f32[32,1,1]{2,1,0:T(1,128)S(1)} all-to-all(f32[32,1,1]{2,1,0:T(1,128)S(1)} %broadcast_in_dim.5), channel_id=1, replica_groups=mesh['grp'=16,'cand'=32] {'cand'}, dimensions={0} | all-to-all | bytes 256 | tf_op jit(solution)/shard_map/all_to_all | solution.py:25
  294.0 0.6 reduce_sum.29
  295.4 0.7 broadcast_multiply_fusion
  (20 shorter events, 0.2 us)
Async XLA Ops:
  7.2 71.0 %copy-start = (bf16[24,32,1024]{2,1,0:T(8,128)(2,1)S(1)}, bf16[24,32,1024]{2,1,0:T(8,128)(2,1)}, u32[]{:S(2)}) copy-start(bf16[24,32,1024]{2,1,0:T(8,128)(2,1)} %param.6) | copy-start | bytes 4718596
  7.2 71.0 %all-gather.2.cloned.1.call-start = ((), (), s32[]{:S(2)}) async-start(), calls=%async_computation.3 | async-start | bytes 4325376 | tf_op jit(solution)/shard_map/all_gather | solution.py:71
  83.5 2.7 copy-start.6
  86.1 8.6 %copy-start.1 = (s32[24,32]{1,0:T(8,128)S(1)}, s32[24,32]{1,0:T(8,128)}, u32[]{:S(2)}) copy-start(s32[24,32]{1,0:T(8,128)} %param.10) | copy-start | bytes 9220
  86.1 8.6 %copy-start.2 = (s32[24,32]{1,0:T(8,128)S(1)}, s32[24,32]{1,0:T(8,128)}, u32[]{:S(2)}) copy-start(s32[24,32]{1,0:T(8,128)} %param.9) | copy-start | bytes 9220
  86.1 8.6 %copy-start.3 = (bf16[2048]{0:T(1024)(128)(2,1)S(1)}, bf16[2048]{0:T(1024)(128)(2,1)}, u32[]{:S(2)}) copy-start(bf16[2048]{0:T(1024)(128)(2,1)} %param.8) | copy-start | bytes 12292
  86.1 17.7 %copy-start.5 = (f32[24]{0:T(128)S(1)}, f32[24]{0:T(128)}, u32[]{:S(2)}) copy-start(f32[24]{0:T(128)} %param.11) | copy-start | bytes 292
  89.3 12.7 %all-to-all-start = ((f32[32,1,768]{2,1,0:T(1,128)}), f32[32,1,768]{2,1,0:T(1,128)S(1)}, u32[]{:S(2)}, u32[]{:S(2)}) async-start(f32[32,1,768]{2,1,0:T(1,128)} %reshape.24), calls=%async_computation | async-start | bytes 196608 | tf_op jit(solution)/shard_map/all_to_all | solution.py:25
  94.6 124.2 %reduce-scatter.2.cloned.1.call-start = ((), (), s32[]{:S(2)}) async-start(), calls=%async_computation.4 | async-start | bytes 4325376 | tf_op jit(solution)/shard_map/reduce_scatter | solution.py:94
  106.8 10.5 %copy-start.4 = (f32[24,32]{1,0:T(8,128)}, f32[24,32]{1,0:T(8,128)S(1)}, u32[]{:S(2)}) copy-start(f32[24,32]{1,0:T(8,128)S(1)} %fusion.13) | copy-start | bytes 9220
Sparse Core Ops, SparseCore 0:
  11.1 67.0 all-gather.1
  117.5 101.2 reduce-scatter.1
where the time goes:
time: 303 us
  waiting for transfers between devices  148 us (49%)
  blocking collectives  102 us (34%)
  matrix products  17.9 us (6%)
  between operations  14.9 us (5%)
  local copies, waits for them, and re-layouts  8.06 us (3%)
  other arithmetic  6.06 us (2%)
  starting transfers between devices  5.38 us (2%)
    reduce_scatter x1, waiting for transfers between devices, per_device(): lax.psum_scatter(lax.dot_general(grad_pre, cand_rows, (((0,), (0,)), ((),...  101 us
    psum x1, blocking collectives, per_device(): summed = lax.psum(owned, 'grp')  46.8 us
    all_gather x1, waiting for transfers between devices, per_device(): lax.all_gather(hidden_weight, 'cand', axis=0, tiled=True)  38.9 us
    all_gather x1, blocking collectives, turned_gather(): result = lax.all_gather(both, axis, axis=0, tiled=True)  28.5 us
    all_to_all x1, blocking collectives, copy_for_each(): return lax.all_to_all(copies, axis, split_axis=0, concat_axis=0, tiled=True)  27.1 us
    dot_general x1, matrix products, per_device(): lax.dot_general(grad_pre, cand_rows, (((0,), (0,)), ((), ())), preferred_...  10.4 us
    all_to_all x1, waiting for transfers between devices, copy_for_each(): return lax.all_to_all(copies, axis, split_axis=0, concat_axis=0, tiled=True)  7.27 us
    unnamed x21, local copies, waits for them, and re-layouts  6.27 us
  transfers between devices with their start and end apart: 3, of which 3 were waited for; matrix products, arithmetic and copies ran while one was open for 1% of the time, Pallas kernels for 0%

commit v1 on v0

--- a/solution.py
+++ b/solution.py
@@ -10,7 +10,9 @@
     turned = [jnp.moveaxis(a, dim, 0) for a, dim in zip(arrays, dims)]
     widths = [t[0].size for t in turned]
     both = jnp.concatenate([t.reshape(-1, w) for t, w in zip(turned, widths)], axis=1)
-    result = lax.all_gather(both, axis, axis=0, tiled=True)
+    vec_out = jnp.stack([both for _ in range(lax.axis_size(axis))], 0)
+    n_now = lax.all_to_all(vec_out, axis_name=axis, split_axis=0, concat_axis=0)
+    result = jnp.concatenate(n_now, 0)
     parts = jnp.split(result, [sum(widths[:k]) for k in range(1, len(widths))], axis=1)
     return tuple(
         (

time: 303 us -> 304 us (level)
  blocking collectives: 102 us -> 73.9 us
  waiting for transfers between devices: 148 us -> 163 us
  starting transfers between devices: 5.38 us -> 15.7 us
  other arithmetic: 6.06 us -> 9.23 us
    all_gather x1 -> x0, blocking collectives: 28.5 us -> none  [turned_gather(): result = lax.all_gather(both, axis, axis=0, tiled=True)]
    all_to_all x0 -> x1, starting transfers between devices: none -> 10.4 us  [turned_gather(): n_now = lax.all_to_all(vec_out, axis_name=axis, split_axis=0, concat_axis=0)]
    all_gather x1, waiting for transfers between devices: 38.9 us -> 47.1 us  [per_device(): lax.all_gather(hidden_weight, 'cand', axis=0, tiled=True)]
    all_to_all x0 -> x1, waiting for transfers between devices: none -> 6.22 us  [turned_gather(): n_now = lax.all_to_all(vec_out, axis_name=axis, split_axis=0, concat_axis=0)]
    unnamed x21 -> x15, local copies, waits for them, and re-layouts: 6.27 us -> 6.11 us
  transfers between devices with their start and end apart: 3 -> 4, of which waited for: 3 -> 4; matrix products, arithmetic and copies ran while one was open for 1% -> 2% of each run, Pallas kernels for 0% -> 0%
where the time goes in v1:
time: 304 us; the launch traced here: 303 us
  waiting for transfers between devices  163 us (54%)
  blocking collectives  73.9 us (24%)
  matrix products  17.9 us (6%)
  starting transfers between devices  15.7 us (5%)
  between operations  14.9 us (5%)
  other arithmetic  9.23 us (3%)
  local copies, waits for them, and re-layouts  8.55 us (3%)
    reduce_scatter x1, waiting for transfers between devices, per_device(): lax.psum_scatter(lax.dot_general(grad_pre, cand_rows, (((0,), (0,)), ((),...  102 us
    all_gather x1, waiting for transfers between devices, per_device(): lax.all_gather(hidden_weight, 'cand', axis=0, tiled=True)  47.1 us
    psum x1, blocking collectives, per_device(): summed = lax.psum(owned, 'grp')  46.6 us
    all_to_all x1, blocking collectives, copy_for_each(): return lax.all_to_all(copies, axis, split_axis=0, concat_axis=0, tiled=True)  27.3 us
    dot_general x1, matrix products, per_device(): lax.dot_general(grad_pre, cand_rows, (((0,), (0,)), ((), ())), preferred_...  10.4 us
    all_to_all x1, starting transfers between devices, turned_gather(): n_now = lax.all_to_all(vec_out, axis_name=axis, split_axis=0, concat_axis=0)  10.4 us
    all_to_all x1, waiting for transfers between devices, copy_for_each(): return lax.all_to_all(copies, axis, split_axis=0, concat_axis=0, tiled=True)  7.28 us
    all_to_all x1, waiting for transfers between devices, turned_gather(): n_now = lax.all_to_all(vec_out, axis_name=axis, split_axis=0, concat_axis=0)  6.22 us
  transfers between devices with their start and end apart: 4, of which 4 were waited for; matrix products, arithmetic and copies ran while one was open for 2% of the time, Pallas kernels for 0%

profile of v1, /device:TPU:1, one launch (start us, length us, event | category | flops | bytes accessed | tf_op | source)
XLA Modules:
  0.0 303.0 jit_solution(16911326191457132690)
XLA Ops:
  7.2 0.7 all-gather.2.cloned.1.call-update
  7.9 0.7 pad_add_fusion
  8.8 1.2 reshape.32
  10.0 10.4 %all-to-all-start = ((s32[32,1,1536]{2,1,0:T(1,128)}), s32[32,1,1536]{2,1,0:T(1,128)S(1)}, u32[]{:S(2)}, u32[]{:S(2)}) async-start(s32[32,1,1536]{2,1,0:T(1,128)} %reshape.32), calls=%async_computation | async-start | bytes 393216 | tf_op jit(solution)/shard_map/all_to_all | solution.py:14
  20.3 0.7 reshape.26
  21.0 0.7 convert_element_type.34
  21.7 0.7 multiply_divide_fusion
  22.5 6.2 %all-to-all-done = s32[32,1,1536]{2,1,0:T(1,128)S(1)} async-done(((s32[32,1,1536]{2,1,0:T(1,128)}), s32[32,1,1536]{2,1,0:T(1,128)S(1)}, u32[]{:S(2)}, u32[]{:S(2)}) %all-to-all-start) | async-done | bytes 196640 | tf_op jit(solution)/shard_map/all_to_all | solution.py:14
  28.7 0.5 broadcast.87
  29.2 1.1 reduce.4
  30.3 0.2 reshape.33
  30.6 0.2 fusion.33
  30.9 0.2 copy.27
  31.1 47.1 %all-gather.2.cloned.1.call-done = bf16[2048,1024]{1,0:T(8,128)(2,1)} async-done(((bf16[64,1024]{1,0:T(8,128)(2,1)}), bf16[2048,1024]{1,0:T(8,128)(2,1)}) %all-gather.2.cloned.1.call-update) | async-done | bytes 4194320 | tf_op jit(solution)/shard_map/all_gather | solution.py:73
  78.2 5.3 %fusion.34 = f32[768,2048]{1,0:T(8,128)S(1)} fusion(bf16[768,1024]{1,0:T(8,128)(2,1)S(1)} %bitcast.13, bf16[2048,1024]{1,0:T(8,128)(2,1)} %all-gather.2.cloned.1.call-done), kind=kOutput, calls=%fused_computation.48 | convolution fusion | flops 3221225472 | bytes 12058624 | tf_op jit(solution)/shard_map/dot_general | solution.py:71
  83.5 2.7 copy-done.3
  86.1 2.2 fusion.22
  88.4 0.8 reshape.30
  89.3 5.3 %all-to-all-start.1 = ((f32[32,1,768]{2,1,0:T(1,128)}), f32[32,1,768]{2,1,0:T(1,128)S(1)}, u32[]{:S(2)}, u32[]{:S(2)}) async-start(f32[32,1,768]{2,1,0:T(1,128)} %reshape.30), calls=%async_computation.1 | async-start | bytes 196608 | tf_op jit(solution)/shard_map/all_to_all | solution.py:27
  94.7 7.3 %all-to-all-done.1 = f32[32,1,768]{2,1,0:T(1,128)S(1)} async-done(((f32[32,1,768]{2,1,0:T(1,128)}), f32[32,1,768]{2,1,0:T(1,128)S(1)}, u32[]{:S(2)}, u32[]{:S(2)}) %all-to-all-start.1) | async-done | bytes 98336 | tf_op jit(solution)/shard_map/all_to_all | solution.py:27
  102.0 0.5 broadcast.86
  102.5 0.9 reduce.3
  103.6 0.2 sub.65
  103.8 3.0 fusion.13
  106.9 10.4 %convolution_convert_fusion = bf16[2048,1024]{1,0:T(8,128)(2,1)} fusion(bf16[768,1024]{1,0:T(8,128)(2,1)S(1)} %bitcast.14, f32[768,2048]{1,0:T(8,128)} %copy-done.3, f32[2048]{0:T(1024)S(1)} %convert_element_type.34, f32[768]{0:T(1024)S(1)} %mul.88), kind=kOutput, calls=%fused_computation.19 | convolution fusion | flops 3256352768 | bytes 12069888 | tf_op jit(solution)/shard_map/dot_general | solution.py:97
  117.3 101.5 %reduce-scatter.2.cloned.1.call-done = bf16[64,1024]{1,0:T(8,128)(2,1)} async-done(((bf16[2048,1024]{1,0:T(8,128)(2,1)}), bf16[64,1024]{1,0:T(8,128)(2,1)}) %reduce-scatter.2.cloned.1.call-update) | async-done | bytes 131088 | tf_op jit(solution)/shard_map/reduce_scatter | solution.py:96
  218.8 46.6 %all-reduce.1 = f32[64,1024]{1,0:T(8,128)S(1)} all-reduce(bf16[64,1024]{1,0:T(8,128)(2,1)} %reduce-scatter.2.cloned.1.call-done), channel_id=1, replica_groups=mesh['grp'=16,'cand'=32] {'grp'}, use_global_device_ids=true, to_apply=%region_2.0 | all-reduce | flops 65536 | bytes 393216 | tf_op jit(solution)/shard_map/psum | solution.py:104
  265.4 0.7 multiply_reduce_fusion
  266.1 0.7 broadcast_in_dim.5
  266.8 27.3 %all_to_all.16 = f32[32,1,1]{2,1,0:T(1,128)S(1)} all-to-all(f32[32,1,1]{2,1,0:T(1,128)S(1)} %broadcast_in_dim.5), channel_id=1, replica_groups=mesh['grp'=16,'cand'=32] {'cand'}, dimensions={0} | all-to-all | bytes 256 | tf_op jit(solution)/shard_map/all_to_all | solution.py:27
  294.1 0.6 reduce_sum.29
  295.4 0.7 broadcast_multiply_fusion
  (19 shorter events, 0.9 us)
Async XLA Ops:
  7.2 71.0 %copy-start = (bf16[24,32,1024]{2,1,0:T(8,128)(2,1)S(1)}, bf16[24,32,1024]{2,1,0:T(8,128)(2,1)}, u32[]{:S(2)}) copy-start(bf16[24,32,1024]{2,1,0:T(8,128)(2,1)} %param.6) | copy-start | bytes 4718596
  7.2 71.0 %all-gather.2.cloned.1.call-start = ((), (), s32[]{:S(2)}) async-start(), calls=%async_computation.4 | async-start | bytes 4325376 | tf_op jit(solution)/shard_map/all_gather | solution.py:73
  10.0 18.7 %all-to-all-start = ((s32[32,1,1536]{2,1,0:T(1,128)}), s32[32,1,1536]{2,1,0:T(1,128)S(1)}, u32[]{:S(2)}, u32[]{:S(2)}) async-start(s32[32,1,1536]{2,1,0:T(1,128)} %reshape.32), calls=%async_computation | async-start | bytes 393216 | tf_op jit(solution)/shard_map/all_to_all | solution.py:14
  83.5 2.7 copy-start.3
  86.1 17.7 %copy-start.2 = (f32[24]{0:T(128)S(1)}, f32[24]{0:T(128)}, u32[]{:S(2)}) copy-start(f32[24]{0:T(128)} %param.11) | copy-start | bytes 292
  89.3 12.7 %all-to-all-start.1 = ((f32[32,1,768]{2,1,0:T(1,128)}), f32[32,1,768]{2,1,0:T(1,128)S(1)}, u32[]{:S(2)}, u32[]{:S(2)}) async-start(f32[32,1,768]{2,1,0:T(1,128)} %reshape.30), calls=%async_computation.1 | async-start | bytes 196608 | tf_op jit(solution)/shard_map/all_to_all | solution.py:27
  94.6 124.2 %reduce-scatter.2.cloned.1.call-start = ((), (), s32[]{:S(2)}) async-start(), calls=%async_computation.5 | async-start | bytes 4325376 | tf_op jit(solution)/shard_map/reduce_scatter | solution.py:96
  106.8 10.5 %copy-start.1 = (f32[24,32]{1,0:T(8,128)}, f32[24,32]{1,0:T(8,128)S(1)}, u32[]{:S(2)}) copy-start(f32[24,32]{1,0:T(8,128)S(1)} %fusion.13) | copy-start | bytes 9220
Sparse Core Ops, SparseCore 0:
  11.1 67.0 all-gather.1
  117.4 101.3 reduce-scatter.1
